TPU v7x, 256 devices: a whole 4x4x8 slice. The times are simulated.
256 devices in a mesh: node: 4 (over x), sx: 16 (over z_hi, y), sy: 4 (over z_lo, core).
Axes of the slice: x: 4, y: 4, z: 8 (z_hi: 4, z_lo: 2; z = z_hi * 2 + z_lo), core: 2. Of those that a mesh axis runs over, the one named last changes fastest.
Arguments:
- previous: float32 [4, 2, 256, 128, 256], P('node', None, 'sx', 'sy'), may hold values from 0 to 1
- feed_rate: float32 [256, 128, 256], P('sx', 'sy'), may hold values from 0.01 to 0.1
- kill_rate: float32 [256, 128, 256], P('sx', 'sy'), may hold values from 0.03 to 0.1
Outputs:
- sections: float32 [4, 2, 256, 128, 256], P('node', None, 'sx', 'sy')
All inputs are finite; a program needn't handle non-finite values.
Results may differ from a plain program's by a relative error of at most 0.00011.
Values sent between devices are 32-bit elements; how exact they have to be, the bound alone decides.
A program may use at most 64 MiB of HBM per device.

v0:
```python
import jax
import jax.numpy as jnp
from jax import lax
from jax.sharding import PartitionSpec as P

SWEEPS = 2
JACOBI = 12


radau_points = [0.088587959512704, 0.409466864440735, 0.787659461760847, 1.0]
time_step = 4.0
diffusion_values = [1.0, 0.5]


def picked(array, axis, root):
    return lax.dynamic_index_in_dim(lax.all_gather(array, axis), root, 0, keepdims=False)


def padded_2(array, sides, width):
    edges = {}
    for axis, dim in sides:
        count, length = (lax.axis_size(axis), array.shape[dim])
        up = [(i, (i + 1) % count) for i in range(count)]
        last = lax.slice_in_dim(array, length - width, length, axis=dim)
        leading = lax.slice_in_dim(array, 0, width, axis=dim)
        edges[dim] = (
            lax.ppermute(last, axis, up),
            lax.ppermute(leading, axis, [(b, a) for a, b in up]),
        )
    done = []
    for _, dim in sides:
        low, high = edges[dim]
        around = [(width, width) if d in done else (0, 0) for d in range(array.ndim)]
        array = jnp.concatenate([jnp.pad(low, around), array, jnp.pad(high, around)], axis=dim)
        done.append(dim)
    return array


def split_up(array, dim, count):
    lengths = array.shape
    blocks = array.reshape(*lengths[:dim], count, lengths[dim] // count, *lengths[dim + 1 :])
    return jnp.moveaxis(blocks, dim, 0)


def sent_and_summed(array, axis, dim):
    count = lax.axis_size(axis)
    blocks = lax.all_to_all(split_up(array, dim, count), axis, 0, 0, tiled=True)
    return jnp.sum(blocks, axis=0)


def padded_3(block, sides, width):
    for axis, dim in sides:
        count = lax.axis_size(axis)
        forward = [(i, i + 1) for i in range(count - 1)]
        forward.append((count - 1, 0))
        backward = [(target, source) for source, target in forward]
        low = lax.ppermute(
            lax.slice_in_dim(block, block.shape[dim] - width, None, axis=dim), axis, forward
        )
        high = lax.ppermute(lax.slice_in_dim(block, 0, width, axis=dim), axis, backward)
        block = jnp.concatenate([low, block, high], axis=dim)
    return block


def collocation():
    count = len(radau_points)
    table = []
    for row in range(count):
        table.append([0.0] * count)
    for column in range(count):
        poly = [1.0]
        denom = 1.0
        for other in range(count):
            if other != column:
                longer = [0.0] * (len(poly) + 1)
                for place in range(len(poly)):
                    longer[place + 1] = longer[place + 1] + poly[place]
                    longer[place] = longer[place] - radau_points[other] * poly[place]
                poly = longer
                denom = denom * (radau_points[column] - radau_points[other])
        for row in range(count):
            point = radau_points[row]
            total = 0.0
            for place in range(len(poly)):
                total = total + poly[place] * point ** (place + 1) / (place + 1)
            table[row][column] = total / denom
    return table


def beside(padded):
    center = padded[:, 1:-1, 1:-1]
    total = padded[:, 2:, 1:-1] + padded[:, :-2, 1:-1]
    total = total + padded[:, 1:-1, 2:] + padded[:, 1:-1, :-2]
    return total + jnp.roll(center, 1, 3) + jnp.roll(center, -1, 3)


def body(previous, feed_rate, kill_rate):
    node_index = lax.axis_index("node")
    qmatrix = jnp.asarray(collocation(), jnp.float32)
    points = jnp.asarray(radau_points, jnp.float32)
    diag_weight = points[node_index]
    diffusion = jnp.asarray(diffusion_values, jnp.float32)[:, None, None, None]
    coef = time_step * diag_weight * diffusion
    start_value = picked(previous[0], "node", len(radau_points) - 1)
    iterate = previous[0]
    for sweep in range(SWEEPS):
        padded = padded_2(iterate, (("sx", 1), ("sy", 2)), 1)
        diff = diffusion * (beside(padded) - 6.0 * iterate)
        upart = iterate[0]
        vpart = iterate[1]
        uvv = upart * vpart * vpart
        react = jnp.stack(
            [-uvv + feed_rate * (1.0 - upart), uvv - (feed_rate + kill_rate) * vpart], 0
        )
        force = diff + react
        weights = qmatrix[:, node_index][:, None, None, None, None]
        section_terms = weights * force[None]
        summed = sent_and_summed(section_terms, "node", 0)[0]
        right_side = start_value + time_step * (summed - diag_weight * diff)
        extended = padded_2(right_side, (("sx", 1), ("sy", 2)), 1)

        def double_turn(turn, current):
            beside_all = padded_3(current, (("sx", 1), ("sy", 2)), 2)
            midway = (extended + coef * beside(beside_all)) / (1.0 + 6.0 * coef)
            return (right_side + coef * beside(midway)) / (1.0 + 6.0 * coef)

        iterate = lax.fori_loop(0, JACOBI // 2, double_turn, iterate)
    return iterate[None]


def solution(mesh):
    return jax.shard_map(
        body,
        mesh=mesh,
        in_specs=(P("node", None, "sx", "sy", None), P("sx", "sy", None), P("sx", "sy", None)),
        out_specs=P("node", None, "sx", "sy", None),
        check_vma=False,
    )
```

profile of v0, /device:TPU:1, one launch (start us, length us, event | category | flops | bytes accessed | tf_op | source)
XLA Modules:
  0.0 478.6 jit_solution(6320649349242898416)
XLA Ops:
  15.6 6.7 %collective-permute-start.8 = (f32[2,1,32,256]{3,2,1,0:T(8,128)S(1)}, f32[2,1,32,256]{3,2,1,0:T(8,128)S(1)}, u32[]{:S(2)}, u32[]{:S(2)}) collective-permute-start(f32[2,1,32,256]{3,2,1,0:T(8,128)S(1)} %get-tuple-element.163), channel_id=1, source_target_pairs={{4,0},{8,4},{12,8},{16,12},{20,16},{24,20},{28,24},{32,28},{36,32}... | collective-permute-start | bytes 196616 | tf_op jit(solution)/shard_map/ppermute | solution.py:28
  30.6 5.0 %all-to-all-start = ((f32[4,1,2,16,32,256]{5,4,3,2,1,0:T(8,128)}), f32[4,1,2,16,32,256]{5,4,3,2,1,0:T(8,128)}, u32[]{:S(2)}, u32[]{:S(2)}) async-start(f32[4,1,2,16,32,256]{5,4,3,2,1,0:T(8,128)} %broadcast_multiply_fusion.3), calls=%async_computation | async-start | bytes 8388608 | tf_op jit(solution)/shard_map/all_to_all | solution.py:47
  36.2 72.7 %all-to-all-done = f32[4,1,2,16,32,256]{5,4,3,2,1,0:T(8,128)} async-done(((f32[4,1,2,16,32,256]{5,4,3,2,1,0:T(8,128)}), f32[4,1,2,16,32,256]{5,4,3,2,1,0:T(8,128)}, u32[]{:S(2)}, u32[]{:S(2)}) %all-to-all-start) | async-done | bytes 4194336 | tf_op jit(solution)/shard_map/all_to_all | solution.py:47
  115.0 5.1 %collective-permute-start.14 = (f32[2,1,32,256]{3,2,1,0:T(8,128)S(1)}, f32[2,1,32,256]{3,2,1,0:T(8,128)S(1)}, u32[]{:S(2)}, u32[]{:S(2)}) collective-permute-start(f32[2,1,32,256]{3,2,1,0:T(8,128)S(1)} %get-tuple-element.157), channel_id=1, source_target_pairs={{4,0},{8,4},{12,8},{16,12},{20,16},{24,20},{28,24},{32,28},{36,32}... | collective-permute-start | bytes 196616 | tf_op jit(solution)/shard_map/ppermute | solution.py:28
  126.8 131.0 %while.22 = (s32[]{:T(128)}, f32[2,16,32,256]{3,2,1,0:T(8,128)S(1)}, f32[2,18,34,256]{3,2,1,0:T(8,128)}, f32[2,16,32,256]{3,2,1,0:T(8,128)S(1)}, f32[]{:T(128)}, /*index=5*/s32[]{:T(128)}, f32[2]{0:T(128)S(1)}) while((s32[]{:T(128)}, f32[2,16,32,256]{3,2,1,0:T(8,128)S(1)}, f32[2,18,34,256]{3,2,1,0:T(8,128)}, ...), condition=%wide.region_2.3_spmd.clone, body=%wide.region_1.2_spmd.clone.sunk | while | flops 7118856 | bytes 39731524 | solution.py:127
  127.0 5.7 %collective-permute-start.1 = (f32[2,2,32,256]{3,2,1,0:T(8,128)S(1)}, f32[2,2,32,256]{3,2,1,0:T(8,128)S(1)}, u32[]{:S(2)}, u32[]{:S(2)}) collective-permute-start(f32[2,2,32,256]{3,2,1,0:T(8,128)S(1)} %get-tuple-element.254), channel_id=1, source_target_pairs={{4,0},{8,4},{12,8},{16,12},{20,16},{24,20},{28,24},{32,28},{36,32}... | collective-permute-start | bytes 393224 | tf_op jit(solution)/shard_map/while/body/eval_jaxpr/ppermute | solution.py:60
  132.6 4.7 collective-permute-done
  148.7 5.7 %collective-permute-start.1 = (f32[2,2,32,256]{3,2,1,0:T(8,128)S(1)}, f32[2,2,32,256]{3,2,1,0:T(8,128)S(1)}, u32[]{:S(2)}, u32[]{:S(2)}) collective-permute-start(f32[2,2,32,256]{3,2,1,0:T(8,128)S(1)} %get-tuple-element.254), channel_id=1, source_target_pairs={{4,0},{8,4},{12,8},{16,12},{20,16},{24,20},{28,24},{32,28},{36,32}... | collective-permute-start | bytes 393224 | tf_op jit(solution)/shard_map/while/body/eval_jaxpr/ppermute | solution.py:60
  154.4 5.0 %collective-permute-done = f32[2,2,32,256]{3,2,1,0:T(8,128)S(1)} collective-permute-done((f32[2,2,32,256]{3,2,1,0:T(8,128)S(1)}, f32[2,2,32,256]{3,2,1,0:T(8,128)S(1)}, u32[]{:S(2)}, u32[]{:S(2)}) %collective-permute-start) | collective-permute-done | bytes 131104 | tf_op jit(solution)/shard_map/while/body/eval_jaxpr/ppermute | solution.py:57
  170.8 5.7 %collective-permute-start.1 = (f32[2,2,32,256]{3,2,1,0:T(8,128)S(1)}, f32[2,2,32,256]{3,2,1,0:T(8,128)S(1)}, u32[]{:S(2)}, u32[]{:S(2)}) collective-permute-start(f32[2,2,32,256]{3,2,1,0:T(8,128)S(1)} %get-tuple-element.254), channel_id=1, source_target_pairs={{4,0},{8,4},{12,8},{16,12},{20,16},{24,20},{28,24},{32,28},{36,32}... | collective-permute-start | bytes 393224 | tf_op jit(solution)/shard_map/while/body/eval_jaxpr/ppermute | solution.py:60
  176.4 4.6 collective-permute-done
  192.5 5.7 %collective-permute-start.1 = (f32[2,2,32,256]{3,2,1,0:T(8,128)S(1)}, f32[2,2,32,256]{3,2,1,0:T(8,128)S(1)}, u32[]{:S(2)}, u32[]{:S(2)}) collective-permute-start(f32[2,2,32,256]{3,2,1,0:T(8,128)S(1)} %get-tuple-element.254), channel_id=1, source_target_pairs={{4,0},{8,4},{12,8},{16,12},{20,16},{24,20},{28,24},{32,28},{36,32}... | collective-permute-start | bytes 393224 | tf_op jit(solution)/shard_map/while/body/eval_jaxpr/ppermute | solution.py:60
  198.2 4.7 collective-permute-done
  214.4 5.7 %collective-permute-start.1 = (f32[2,2,32,256]{3,2,1,0:T(8,128)S(1)}, f32[2,2,32,256]{3,2,1,0:T(8,128)S(1)}, u32[]{:S(2)}, u32[]{:S(2)}) collective-permute-start(f32[2,2,32,256]{3,2,1,0:T(8,128)S(1)} %get-tuple-element.254), channel_id=1, source_target_pairs={{4,0},{8,4},{12,8},{16,12},{20,16},{24,20},{28,24},{32,28},{36,32}... | collective-permute-start | bytes 393224 | tf_op jit(solution)/shard_map/while/body/eval_jaxpr/ppermute | solution.py:60
  220.1 4.2 collective-permute-done
  236.3 5.7 %collective-permute-start.1 = (f32[2,2,32,256]{3,2,1,0:T(8,128)S(1)}, f32[2,2,32,256]{3,2,1,0:T(8,128)S(1)}, u32[]{:S(2)}, u32[]{:S(2)}) collective-permute-start(f32[2,2,32,256]{3,2,1,0:T(8,128)S(1)} %get-tuple-element.254), channel_id=1, source_target_pairs={{4,0},{8,4},{12,8},{16,12},{20,16},{24,20},{28,24},{32,28},{36,32}... | collective-permute-start | bytes 393224 | tf_op jit(solution)/shard_map/while/body/eval_jaxpr/ppermute | solution.py:60
  242.0 3.7 collective-permute-done
  260.6 5.8 %collective-permute-start.16 = (f32[2,1,32,256]{3,2,1,0:T(8,128)S(1)}, f32[2,1,32,256]{3,2,1,0:T(8,128)S(1)}, u32[]{:S(2)}, u32[]{:S(2)}) collective-permute-start(f32[2,1,32,256]{3,2,1,0:T(8,128)S(1)} %get-tuple-element.148), channel_id=1, source_target_pairs={{4,0},{8,4},{12,8},{16,12},{20,16},{24,20},{28,24},{32,28},{36,32}... | collective-permute-start | bytes 196616 | tf_op jit(solution)/shard_map/ppermute | solution.py:28
  271.0 52.0 %all_to_all.10 = f32[4,1,2,16,32,256]{5,4,3,2,1,0:T(8,128)} all-to-all(f32[4,1,2,16,32,256]{5,4,3,2,1,0:T(8,128)S(1)} %broadcast_multiply_fusion.2), channel_id=1, replica_groups=mesh['node'=4,'sx'=16,'sy'=4] {'node'}, dimensions={0} | all-to-all | bytes 8388608 | tf_op jit(solution)/shard_map/all_to_all | solution.py:47
  323.0 3.7 reduce_sum.19
  329.2 6.2 %collective-permute-start.22 = (f32[2,1,32,256]{3,2,1,0:T(8,128)S(1)}, f32[2,1,32,256]{3,2,1,0:T(8,128)S(1)}, u32[]{:S(2)}, u32[]{:S(2)}) collective-permute-start(f32[2,1,32,256]{3,2,1,0:T(8,128)S(1)} %get-tuple-element.143), channel_id=1, source_target_pairs={{4,0},{8,4},{12,8},{16,12},{20,16},{24,20},{28,24},{32,28},{36,32}... | collective-permute-start | bytes 196616 | tf_op jit(solution)/shard_map/ppermute | solution.py:28
  342.1 128.7 %while.23 = (s32[]{:T(128)}, f32[2,16,32,256]{3,2,1,0:T(8,128)S(1)}, f32[2,18,34,256]{3,2,1,0:T(8,128)}, f32[2,16,32,256]{3,2,1,0:T(8,128)S(1)}, f32[]{:T(128)}, /*index=5*/s32[]{:T(128)}, f32[2]{0:T(128)S(1)}) while((s32[]{:T(128)}, f32[2,16,32,256]{3,2,1,0:T(8,128)S(1)}, f32[2,18,34,256]{3,2,1,0:T(8,128)}, ...), condition=%wide.region_5.6_spmd.clone, body=%wide.region_4.5_spmd.clone.sunk | while | flops 7118856 | bytes 39731524 | solution.py:127
  342.2 5.7 %collective-permute-start.5 = (f32[2,2,32,256]{3,2,1,0:T(8,128)S(1)}, f32[2,2,32,256]{3,2,1,0:T(8,128)S(1)}, u32[]{:S(2)}, u32[]{:S(2)}) collective-permute-start(f32[2,2,32,256]{3,2,1,0:T(8,128)S(1)} %get-tuple-element.273), channel_id=1, source_target_pairs={{4,0},{8,4},{12,8},{16,12},{20,16},{24,20},{28,24},{32,28},{36,32}... | collective-permute-start | bytes 393224 | tf_op jit(solution)/shard_map/while/body/eval_jaxpr/ppermute | solution.py:60
  347.9 4.0 collective-permute-done.4
  363.9 6.0 %collective-permute-start.5 = (f32[2,2,32,256]{3,2,1,0:T(8,128)S(1)}, f32[2,2,32,256]{3,2,1,0:T(8,128)S(1)}, u32[]{:S(2)}, u32[]{:S(2)}) collective-permute-start(f32[2,2,32,256]{3,2,1,0:T(8,128)S(1)} %get-tuple-element.273), channel_id=1, source_target_pairs={{4,0},{8,4},{12,8},{16,12},{20,16},{24,20},{28,24},{32,28},{36,32}... | collective-permute-start | bytes 393224 | tf_op jit(solution)/shard_map/while/body/eval_jaxpr/ppermute | solution.py:60
  385.1 5.8 %collective-permute-start.5 = (f32[2,2,32,256]{3,2,1,0:T(8,128)S(1)}, f32[2,2,32,256]{3,2,1,0:T(8,128)S(1)}, u32[]{:S(2)}, u32[]{:S(2)}) collective-permute-start(f32[2,2,32,256]{3,2,1,0:T(8,128)S(1)} %get-tuple-element.273), channel_id=1, source_target_pairs={{4,0},{8,4},{12,8},{16,12},{20,16},{24,20},{28,24},{32,28},{36,32}... | collective-permute-start | bytes 393224 | tf_op jit(solution)/shard_map/while/body/eval_jaxpr/ppermute | solution.py:60
  398.5 3.5 collective-permute-done.7
  406.5 5.7 %collective-permute-start.5 = (f32[2,2,32,256]{3,2,1,0:T(8,128)S(1)}, f32[2,2,32,256]{3,2,1,0:T(8,128)S(1)}, u32[]{:S(2)}, u32[]{:S(2)}) collective-permute-start(f32[2,2,32,256]{3,2,1,0:T(8,128)S(1)} %get-tuple-element.273), channel_id=1, source_target_pairs={{4,0},{8,4},{12,8},{16,12},{20,16},{24,20},{28,24},{32,28},{36,32}... | collective-permute-start | bytes 393224 | tf_op jit(solution)/shard_map/while/body/eval_jaxpr/ppermute | solution.py:60
  427.3 6.7 %collective-permute-start.5 = (f32[2,2,32,256]{3,2,1,0:T(8,128)S(1)}, f32[2,2,32,256]{3,2,1,0:T(8,128)S(1)}, u32[]{:S(2)}, u32[]{:S(2)}) collective-permute-start(f32[2,2,32,256]{3,2,1,0:T(8,128)S(1)} %get-tuple-element.273), channel_id=1, source_target_pairs={{4,0},{8,4},{12,8},{16,12},{20,16},{24,20},{28,24},{32,28},{36,32}... | collective-permute-start | bytes 393224 | tf_op jit(solution)/shard_map/while/body/eval_jaxpr/ppermute | solution.py:60
  434.0 3.4 collective-permute-done.4
  441.5 3.5 collective-permute-done.7
  449.5 6.3 %collective-permute-start.5 = (f32[2,2,32,256]{3,2,1,0:T(8,128)S(1)}, f32[2,2,32,256]{3,2,1,0:T(8,128)S(1)}, u32[]{:S(2)}, u32[]{:S(2)}) collective-permute-start(f32[2,2,32,256]{3,2,1,0:T(8,128)S(1)} %get-tuple-element.273), channel_id=1, source_target_pairs={{4,0},{8,4},{12,8},{16,12},{20,16},{24,20},{28,24},{32,28},{36,32}... | collective-permute-start | bytes 393224 | tf_op jit(solution)/shard_map/while/body/eval_jaxpr/ppermute | solution.py:60
  (330 shorter events, 194.6 us)
Async XLA Ops:
  6.5 105.1 %all-gather.2.cloned.1.call-start = ((), (), s32[]{:S(2)}) async-start(), calls=%async_computation.2 | async-start | bytes 5242880 | tf_op jit(solution)/shard_map/all_gather | solution.py:16
  10.1 14.5 %collective-permute-start.10 = (f32[2,16,1,256]{3,2,1,0:T(1,128)S(1)}, f32[2,16,1,256]{3,2,1,0:T(1,128)S(1)}, u32[]{:S(2)}, u32[]{:S(2)}) collective-permute-start(f32[2,16,1,256]{3,2,1,0:T(1,128)S(1)} %get-tuple-element.160), channel_id=1, source_target_pairs={{1,0},{2,1},{3,2},{0,3},{5,4},{6,5},{7,6},{4,7},{9,8},{10,9},{11,1... | collective-permute-start | bytes 98312 | tf_op jit(solution)/shard_map/ppermute | solution.py:28
  13.4 11.2 %collective-permute-start.11 = (f32[2,16,1,256]{3,2,1,0:T(1,128)S(1)}, f32[2,16,1,256]{3,2,1,0:T(1,128)S(1)}, u32[]{:S(2)}, u32[]{:S(2)}) collective-permute-start(f32[2,16,1,256]{3,2,1,0:T(1,128)S(1)} %get-tuple-element.161), channel_id=1, source_target_pairs={{0,1},{1,2},{2,3},{3,0},{4,5},{5,6},{6,7},{7,4},{8,9},{9,10},{10,1... | collective-permute-start | bytes 98312 | tf_op jit(solution)/shard_map/ppermute | solution.py:27
  14.3 10.3 %collective-permute-start.9 = (f32[2,1,32,256]{3,2,1,0:T(8,128)S(1)}, f32[2,1,32,256]{3,2,1,0:T(8,128)S(1)}, u32[]{:S(2)}, u32[]{:S(2)}) collective-permute-start(f32[2,1,32,256]{3,2,1,0:T(8,128)S(1)} %get-tuple-element.162), channel_id=1, source_target_pairs={{0,4},{4,8},{8,12},{12,16},{16,20},{20,24},{24,28},{28,32},{32,36}... | collective-permute-start | bytes 196616 | tf_op jit(solution)/shard_map/ppermute | solution.py:27
  15.6 10.0 %collective-permute-start.8 = (f32[2,1,32,256]{3,2,1,0:T(8,128)S(1)}, f32[2,1,32,256]{3,2,1,0:T(8,128)S(1)}, u32[]{:S(2)}, u32[]{:S(2)}) collective-permute-start(f32[2,1,32,256]{3,2,1,0:T(8,128)S(1)} %get-tuple-element.163), channel_id=1, source_target_pairs={{4,0},{8,4},{12,8},{16,12},{20,16},{24,20},{28,24},{32,28},{36,32}... | collective-permute-start | bytes 196616 | tf_op jit(solution)/shard_map/ppermute | solution.py:28
  30.6 78.3 %all-to-all-start = ((f32[4,1,2,16,32,256]{5,4,3,2,1,0:T(8,128)}), f32[4,1,2,16,32,256]{5,4,3,2,1,0:T(8,128)}, u32[]{:S(2)}, u32[]{:S(2)}) async-start(f32[4,1,2,16,32,256]{5,4,3,2,1,0:T(8,128)} %broadcast_multiply_fusion.3), calls=%async_computation | async-start | bytes 8388608 | tf_op jit(solution)/shard_map/all_to_all | solution.py:47
  114.1 11.4 %collective-permute-start.13 = (f32[2,1,32,256]{3,2,1,0:T(8,128)S(1)}, f32[2,1,32,256]{3,2,1,0:T(8,128)S(1)}, u32[]{:S(2)}, u32[]{:S(2)}) collective-permute-start(f32[2,1,32,256]{3,2,1,0:T(8,128)S(1)} %get-tuple-element.156), channel_id=1, source_target_pairs={{0,4},{4,8},{8,12},{12,16},{16,20},{20,24},{24,28},{28,32},{32,36}... | collective-permute-start | bytes 196616 | tf_op jit(solution)/shard_map/ppermute | solution.py:27
  115.0 10.5 %collective-permute-start.14 = (f32[2,1,32,256]{3,2,1,0:T(8,128)S(1)}, f32[2,1,32,256]{3,2,1,0:T(8,128)S(1)}, u32[]{:S(2)}, u32[]{:S(2)}) collective-permute-start(f32[2,1,32,256]{3,2,1,0:T(8,128)S(1)} %get-tuple-element.157), channel_id=1, source_target_pairs={{4,0},{8,4},{12,8},{16,12},{20,16},{24,20},{28,24},{32,28},{36,32}... | collective-permute-start | bytes 196616 | tf_op jit(solution)/shard_map/ppermute | solution.py:28
  126.9 10.4 %collective-permute-start = (f32[2,2,32,256]{3,2,1,0:T(8,128)S(1)}, f32[2,2,32,256]{3,2,1,0:T(8,128)S(1)}, u32[]{:S(2)}, u32[]{:S(2)}) collective-permute-start(f32[2,2,32,256]{3,2,1,0:T(8,128)S(1)} %get-tuple-element.253), channel_id=1, source_target_pairs={{0,4},{4,8},{8,12},{12,16},{16,20},{20,24},{24,28},{28,32},{32,36}... | collective-permute-start | bytes 393224 | tf_op jit(solution)/shard_map/while/body/eval_jaxpr/ppermute | solution.py:57
  127.0 11.2 %collective-permute-start.1 = (f32[2,2,32,256]{3,2,1,0:T(8,128)S(1)}, f32[2,2,32,256]{3,2,1,0:T(8,128)S(1)}, u32[]{:S(2)}, u32[]{:S(2)}) collective-permute-start(f32[2,2,32,256]{3,2,1,0:T(8,128)S(1)} %get-tuple-element.254), channel_id=1, source_target_pairs={{4,0},{8,4},{12,8},{16,12},{20,16},{24,20},{28,24},{32,28},{36,32}... | collective-permute-start | bytes 393224 | tf_op jit(solution)/shard_map/while/body/eval_jaxpr/ppermute | solution.py:60
  148.6 10.8 %collective-permute-start = (f32[2,2,32,256]{3,2,1,0:T(8,128)S(1)}, f32[2,2,32,256]{3,2,1,0:T(8,128)S(1)}, u32[]{:S(2)}, u32[]{:S(2)}) collective-permute-start(f32[2,2,32,256]{3,2,1,0:T(8,128)S(1)} %get-tuple-element.253), channel_id=1, source_target_pairs={{0,4},{4,8},{8,12},{12,16},{16,20},{20,24},{24,28},{28,32},{32,36}... | collective-permute-start | bytes 393224 | tf_op jit(solution)/shard_map/while/body/eval_jaxpr/ppermute | solution.py:57
  148.7 10.8 %collective-permute-start.1 = (f32[2,2,32,256]{3,2,1,0:T(8,128)S(1)}, f32[2,2,32,256]{3,2,1,0:T(8,128)S(1)}, u32[]{:S(2)}, u32[]{:S(2)}) collective-permute-start(f32[2,2,32,256]{3,2,1,0:T(8,128)S(1)} %get-tuple-element.254), channel_id=1, source_target_pairs={{4,0},{8,4},{12,8},{16,12},{20,16},{24,20},{28,24},{32,28},{36,32}... | collective-permute-start | bytes 393224 | tf_op jit(solution)/shard_map/while/body/eval_jaxpr/ppermute | solution.py:60
  170.7 10.3 %collective-permute-start = (f32[2,2,32,256]{3,2,1,0:T(8,128)S(1)}, f32[2,2,32,256]{3,2,1,0:T(8,128)S(1)}, u32[]{:S(2)}, u32[]{:S(2)}) collective-permute-start(f32[2,2,32,256]{3,2,1,0:T(8,128)S(1)} %get-tuple-element.253), channel_id=1, source_target_pairs={{0,4},{4,8},{8,12},{12,16},{16,20},{20,24},{24,28},{28,32},{32,36}... | collective-permute-start | bytes 393224 | tf_op jit(solution)/shard_map/while/body/eval_jaxpr/ppermute | solution.py:57
  170.8 10.4 %collective-permute-start.1 = (f32[2,2,32,256]{3,2,1,0:T(8,128)S(1)}, f32[2,2,32,256]{3,2,1,0:T(8,128)S(1)}, u32[]{:S(2)}, u32[]{:S(2)}) collective-permute-start(f32[2,2,32,256]{3,2,1,0:T(8,128)S(1)} %get-tuple-element.254), channel_id=1, source_target_pairs={{4,0},{8,4},{12,8},{16,12},{20,16},{24,20},{28,24},{32,28},{36,32}... | collective-permute-start | bytes 393224 | tf_op jit(solution)/shard_map/while/body/eval_jaxpr/ppermute | solution.py:60
  192.4 10.4 %collective-permute-start = (f32[2,2,32,256]{3,2,1,0:T(8,128)S(1)}, f32[2,2,32,256]{3,2,1,0:T(8,128)S(1)}, u32[]{:S(2)}, u32[]{:S(2)}) collective-permute-start(f32[2,2,32,256]{3,2,1,0:T(8,128)S(1)} %get-tuple-element.253), channel_id=1, source_target_pairs={{0,4},{4,8},{8,12},{12,16},{16,20},{20,24},{24,28},{28,32},{32,36}... | collective-permute-start | bytes 393224 | tf_op jit(solution)/shard_map/while/body/eval_jaxpr/ppermute | solution.py:57
  192.5 11.3 %collective-permute-start.1 = (f32[2,2,32,256]{3,2,1,0:T(8,128)S(1)}, f32[2,2,32,256]{3,2,1,0:T(8,128)S(1)}, u32[]{:S(2)}, u32[]{:S(2)}) collective-permute-start(f32[2,2,32,256]{3,2,1,0:T(8,128)S(1)} %get-tuple-element.254), channel_id=1, source_target_pairs={{4,0},{8,4},{12,8},{16,12},{20,16},{24,20},{28,24},{32,28},{36,32}... | collective-permute-start | bytes 393224 | tf_op jit(solution)/shard_map/while/body/eval_jaxpr/ppermute | solution.py:60
  214.3 10.0 %collective-permute-start = (f32[2,2,32,256]{3,2,1,0:T(8,128)S(1)}, f32[2,2,32,256]{3,2,1,0:T(8,128)S(1)}, u32[]{:S(2)}, u32[]{:S(2)}) collective-permute-start(f32[2,2,32,256]{3,2,1,0:T(8,128)S(1)} %get-tuple-element.253), channel_id=1, source_target_pairs={{0,4},{4,8},{8,12},{12,16},{16,20},{20,24},{24,28},{28,32},{32,36}... | collective-permute-start | bytes 393224 | tf_op jit(solution)/shard_map/while/body/eval_jaxpr/ppermute | solution.py:57
  214.4 11.3 %collective-permute-start.1 = (f32[2,2,32,256]{3,2,1,0:T(8,128)S(1)}, f32[2,2,32,256]{3,2,1,0:T(8,128)S(1)}, u32[]{:S(2)}, u32[]{:S(2)}) collective-permute-start(f32[2,2,32,256]{3,2,1,0:T(8,128)S(1)} %get-tuple-element.254), channel_id=1, source_target_pairs={{4,0},{8,4},{12,8},{16,12},{20,16},{24,20},{28,24},{32,28},{36,32}... | collective-permute-start | bytes 393224 | tf_op jit(solution)/shard_map/while/body/eval_jaxpr/ppermute | solution.py:60
  236.2 9.4 %collective-permute-start = (f32[2,2,32,256]{3,2,1,0:T(8,128)S(1)}, f32[2,2,32,256]{3,2,1,0:T(8,128)S(1)}, u32[]{:S(2)}, u32[]{:S(2)}) collective-permute-start(f32[2,2,32,256]{3,2,1,0:T(8,128)S(1)} %get-tuple-element.253), channel_id=1, source_target_pairs={{0,4},{4,8},{8,12},{12,16},{16,20},{20,24},{24,28},{28,32},{32,36}... | collective-permute-start | bytes 393224 | tf_op jit(solution)/shard_map/while/body/eval_jaxpr/ppermute | solution.py:57
  236.3 11.2 %collective-permute-start.1 = (f32[2,2,32,256]{3,2,1,0:T(8,128)S(1)}, f32[2,2,32,256]{3,2,1,0:T(8,128)S(1)}, u32[]{:S(2)}, u32[]{:S(2)}) collective-permute-start(f32[2,2,32,256]{3,2,1,0:T(8,128)S(1)} %get-tuple-element.254), channel_id=1, source_target_pairs={{4,0},{8,4},{12,8},{16,12},{20,16},{24,20},{28,24},{32,28},{36,32}... | collective-permute-start | bytes 393224 | tf_op jit(solution)/shard_map/while/body/eval_jaxpr/ppermute | solution.py:60
  258.3 11.2 %collective-permute-start.18 = (f32[2,16,1,256]{3,2,1,0:T(1,128)S(1)}, f32[2,16,1,256]{3,2,1,0:T(1,128)S(1)}, u32[]{:S(2)}, u32[]{:S(2)}) collective-permute-start(f32[2,16,1,256]{3,2,1,0:T(1,128)S(1)} %get-tuple-element.146), channel_id=1, source_target_pairs={{1,0},{2,1},{3,2},{0,3},{5,4},{6,5},{7,6},{4,7},{9,8},{10,9},{11,1... | collective-permute-start | bytes 98312 | tf_op jit(solution)/shard_map/ppermute | solution.py:28
  258.4 11.1 %collective-permute-start.19 = (f32[2,16,1,256]{3,2,1,0:T(1,128)S(1)}, f32[2,16,1,256]{3,2,1,0:T(1,128)S(1)}, u32[]{:S(2)}, u32[]{:S(2)}) collective-permute-start(f32[2,16,1,256]{3,2,1,0:T(1,128)S(1)} %get-tuple-element.147), channel_id=1, source_target_pairs={{0,1},{1,2},{2,3},{3,0},{4,5},{5,6},{6,7},{7,4},{8,9},{9,10},{10,1... | collective-permute-start | bytes 98312 | tf_op jit(solution)/shard_map/ppermute | solution.py:27
  329.1 11.6 %collective-permute-start.21 = (f32[2,1,32,256]{3,2,1,0:T(8,128)S(1)}, f32[2,1,32,256]{3,2,1,0:T(8,128)S(1)}, u32[]{:S(2)}, u32[]{:S(2)}) collective-permute-start(f32[2,1,32,256]{3,2,1,0:T(8,128)S(1)} %get-tuple-element.142), channel_id=1, source_target_pairs={{0,4},{4,8},{8,12},{12,16},{16,20},{20,24},{24,28},{28,32},{32,36}... | collective-permute-start | bytes 196616 | tf_op jit(solution)/shard_map/ppermute | solution.py:27
  329.2 11.6 %collective-permute-start.22 = (f32[2,1,32,256]{3,2,1,0:T(8,128)S(1)}, f32[2,1,32,256]{3,2,1,0:T(8,128)S(1)}, u32[]{:S(2)}, u32[]{:S(2)}) collective-permute-start(f32[2,1,32,256]{3,2,1,0:T(8,128)S(1)} %get-tuple-element.143), channel_id=1, source_target_pairs={{4,0},{8,4},{12,8},{16,12},{20,16},{24,20},{28,24},{32,28},{36,32}... | collective-permute-start | bytes 196616 | tf_op jit(solution)/shard_map/ppermute | solution.py:28
  342.1 9.7 %collective-permute-start.4 = (f32[2,2,32,256]{3,2,1,0:T(8,128)S(1)}, f32[2,2,32,256]{3,2,1,0:T(8,128)S(1)}, u32[]{:S(2)}, u32[]{:S(2)}) collective-permute-start(f32[2,2,32,256]{3,2,1,0:T(8,128)S(1)} %get-tuple-element.272), channel_id=1, source_target_pairs={{0,4},{4,8},{8,12},{12,16},{16,20},{20,24},{24,28},{28,32},{32,36}... | collective-permute-start | bytes 393224 | tf_op jit(solution)/shard_map/while/body/eval_jaxpr/ppermute | solution.py:57
  342.2 11.4 %collective-permute-start.5 = (f32[2,2,32,256]{3,2,1,0:T(8,128)S(1)}, f32[2,2,32,256]{3,2,1,0:T(8,128)S(1)}, u32[]{:S(2)}, u32[]{:S(2)}) collective-permute-start(f32[2,2,32,256]{3,2,1,0:T(8,128)S(1)} %get-tuple-element.273), channel_id=1, source_target_pairs={{4,0},{8,4},{12,8},{16,12},{20,16},{24,20},{28,24},{32,28},{36,32}... | collective-permute-start | bytes 393224 | tf_op jit(solution)/shard_map/while/body/eval_jaxpr/ppermute | solution.py:60
  363.9 9.7 %collective-permute-start.5 = (f32[2,2,32,256]{3,2,1,0:T(8,128)S(1)}, f32[2,2,32,256]{3,2,1,0:T(8,128)S(1)}, u32[]{:S(2)}, u32[]{:S(2)}) collective-permute-start(f32[2,2,32,256]{3,2,1,0:T(8,128)S(1)} %get-tuple-element.273), channel_id=1, source_target_pairs={{4,0},{8,4},{12,8},{16,12},{20,16},{24,20},{28,24},{32,28},{36,32}... | collective-permute-start | bytes 393224 | tf_op jit(solution)/shard_map/while/body/eval_jaxpr/ppermute | solution.py:60
  406.5 11.3 %collective-permute-start.5 = (f32[2,2,32,256]{3,2,1,0:T(8,128)S(1)}, f32[2,2,32,256]{3,2,1,0:T(8,128)S(1)}, u32[]{:S(2)}, u32[]{:S(2)}) collective-permute-start(f32[2,2,32,256]{3,2,1,0:T(8,128)S(1)} %get-tuple-element.273), channel_id=1, source_target_pairs={{4,0},{8,4},{12,8},{16,12},{20,16},{24,20},{28,24},{32,28},{36,32}... | collective-permute-start | bytes 393224 | tf_op jit(solution)/shard_map/while/body/eval_jaxpr/ppermute | solution.py:60
  427.3 10.1 %collective-permute-start.4 = (f32[2,2,32,256]{3,2,1,0:T(8,128)S(1)}, f32[2,2,32,256]{3,2,1,0:T(8,128)S(1)}, u32[]{:S(2)}, u32[]{:S(2)}) collective-permute-start(f32[2,2,32,256]{3,2,1,0:T(8,128)S(1)} %get-tuple-element.272), channel_id=1, source_target_pairs={{0,4},{4,8},{8,12},{12,16},{16,20},{20,24},{24,28},{28,32},{32,36}... | collective-permute-start | bytes 393224 | tf_op jit(solution)/shard_map/while/body/eval_jaxpr/ppermute | solution.py:57
  427.3 12.3 %collective-permute-start.5 = (f32[2,2,32,256]{3,2,1,0:T(8,128)S(1)}, f32[2,2,32,256]{3,2,1,0:T(8,128)S(1)}, u32[]{:S(2)}, u32[]{:S(2)}) collective-permute-start(f32[2,2,32,256]{3,2,1,0:T(8,128)S(1)} %get-tuple-element.273), channel_id=1, source_target_pairs={{4,0},{8,4},{12,8},{16,12},{20,16},{24,20},{28,24},{32,28},{36,32}... | collective-permute-start | bytes 393224 | tf_op jit(solution)/shard_map/while/body/eval_jaxpr/ppermute | solution.py:60
  449.4 9.7 %collective-permute-start.4 = (f32[2,2,32,256]{3,2,1,0:T(8,128)S(1)}, f32[2,2,32,256]{3,2,1,0:T(8,128)S(1)}, u32[]{:S(2)}, u32[]{:S(2)}) collective-permute-start(f32[2,2,32,256]{3,2,1,0:T(8,128)S(1)} %get-tuple-element.272), channel_id=1, source_target_pairs={{0,4},{4,8},{8,12},{12,16},{16,20},{20,24},{24,28},{28,32},{32,36}... | collective-permute-start | bytes 393224 | tf_op jit(solution)/shard_map/while/body/eval_jaxpr/ppermute | solution.py:57
  449.5 12.3 %collective-permute-start.5 = (f32[2,2,32,256]{3,2,1,0:T(8,128)S(1)}, f32[2,2,32,256]{3,2,1,0:T(8,128)S(1)}, u32[]{:S(2)}, u32[]{:S(2)}) collective-permute-start(f32[2,2,32,256]{3,2,1,0:T(8,128)S(1)} %get-tuple-element.273), channel_id=1, source_target_pairs={{4,0},{8,4},{12,8},{16,12},{20,16},{24,20},{28,24},{32,28},{36,32}... | collective-permute-start | bytes 393224 | tf_op jit(solution)/shard_map/while/body/eval_jaxpr/ppermute | solution.py:60
  (54 other events, 228.6 us)
Sparse Core Ops, SparseCore 0:
  9.1 77.7 all-gather.1
where the time goes:
time: 482 us; the launch traced here: 479 us
  waiting for transfers between devices  191 us (40%)
  starting transfers between devices  136 us (28%)
  blocking collectives  52 us (11%)
  other arithmetic  46.1 us (10%)
  local copies, waits for them, and re-layouts  37.5 us (8%)
  between operations  14.2 us (3%)
    ppermute x24, starting transfers between devices, padded_3(): lax.ppermute(lax.slice_in_dim(block, 0, width, axis=dim), axis, backward)  74.2 us
    all_to_all x1, waiting for transfers between devices, sent_and_summed(): blocks = lax.all_to_all(split_up(array, dim, count), axis, 0, 0, tiled=True)  72.7 us
    ppermute x24, waiting for transfers between devices, padded_3(): lax.ppermute(lax.slice_in_dim(block, block.shape[dim] - width, None, axis...  63.7 us
    all_to_all x1, blocking collectives, sent_and_summed(): blocks = lax.all_to_all(split_up(array, dim, count), axis, 0, 0, tiled=True)  52 us
    ppermute x24, waiting for transfers between devices, padded_3(): lax.ppermute(lax.slice_in_dim(block, 0, width, axis=dim), axis, backward)  44.9 us
    ppermute x8, starting transfers between devices, padded_2(): lax.ppermute(leading, axis, [(b, a) for a, b in up])  27.1 us
    ppermute x24, starting transfers between devices, padded_3(): lax.ppermute(lax.slice_in_dim(block, block.shape[dim] - width, None, axis...  21.9 us
    slice x52, local copies, waits for them, and re-layouts, beside(): return total + jnp.roll(center, 1, 3) + jnp.roll(center, -1, 3)  18.7 us
  transfers between devices with their start and end apart: 66, of which 54 were waited for; matrix products, arithmetic and copies ran while one was open for 3% of the time, Pallas kernels for 0%

commit v1 on v0

v1 whole, which is shorter than its diff:
```python
import jax
import jax.numpy as jnp
from jax import lax
from jax.experimental import pallas as pl
from jax.experimental.pallas import tpu as pltpu
from jax.sharding import PartitionSpec as P

SWEEPS = 2
ROUNDS = 3
W = 4
NA, NB, NC = 16, 32, 256
PA, PB = NA + 2 * W, NB + 2 * W
NODES = 4
SLAB = NA // NODES
MESH = pl.DeviceIdType.MESH

radau_points = [0.088587959512704, 0.409466864440735, 0.787659461760847, 1.0]
time_step = 4.0
diffusion_values = [1.0, 0.5]


def collocation():
    count = len(radau_points)
    table = []
    for row in range(count):
        table.append([0.0] * count)
    for column in range(count):
        poly = [1.0]
        denom = 1.0
        for other in range(count):
            if other != column:
                longer = [0.0] * (len(poly) + 1)
                for place in range(len(poly)):
                    longer[place + 1] = longer[place + 1] + poly[place]
                    longer[place] = longer[place] - radau_points[other] * poly[place]
                poly = longer
                denom = denom * (radau_points[column] - radau_points[other])
        for row in range(count):
            point = radau_points[row]
            total = 0.0
            for place in range(len(poly)):
                total = total + poly[place] * point ** (place + 1) / (place + 1)
            table[row][column] = total / denom
    return table


def chosen(index, values):
    result = jnp.float32(values[-1])
    for place in range(len(values) - 2, -1, -1):
        result = jnp.where(index == place, jnp.float32(values[place]), result)
    return result


def kernel(prev, feed, kill, out, x, g, t, diff, fsend, frecv, rsend, rrecv, start,
           bsend, brecv, hs, hr, as_, ar, ss, sr):
    node = lax.axis_index("node")
    sx = lax.axis_index("sx")
    sy = lax.axis_index("sy")
    nsx = lax.axis_size("sx")
    nsy = lax.axis_size("sy")
    sx_dev = [lax.rem(sx + nsx - 1, nsx), lax.rem(sx + 1, nsx)]
    sy_dev = [lax.rem(sy + nsy - 1, nsy), lax.rem(sy + 1, nsy)]
    peers = {d: lax.rem(node + d, NODES) for d in range(NODES)}
    sources = {d: lax.rem(node + NODES - d, NODES) for d in range(NODES)}

    qmatrix = collocation()
    h_tau = chosen(node, [time_step * p for p in radau_points])
    coefs = [[time_step * p * d for p in radau_points] for d in diffusion_values]
    inv = [chosen(node, [1.0 / (1.0 + 6.0 * c) for c in cs]) for cs in coefs]
    ratio = [chosen(node, [c / (1.0 + 6.0 * c) for c in cs]) for cs in coefs]

    barrier = pltpu.get_barrier_semaphore()
    others = [{"node": peers[d]} for d in (1, 2, 3)]
    others += [{"sx": p} for p in sx_dev] + [{"sy": p} for p in sy_dev]
    for other in others:
        pl.semaphore_signal(barrier, inc=1, device_id=other, device_id_type=MESH)

    low = lax.broadcasted_iota(jnp.int32, (8, NC), 0) < W

    def loop(count, fn):
        def step(i, carry):
            fn(i)
            return carry
        lax.fori_loop(0, count, step, 0)

    def a_copy(ref, at, e, s, way, width):
        src = W if way == 0 else W + NA - width
        dst = W + NA if way == 0 else W - width
        return pltpu.make_async_remote_copy(
            src_ref=ref.at[at, s, pl.ds(src, width), pl.ds(0, NB), :],
            dst_ref=ref.at[at, s, pl.ds(dst, width), pl.ds(0, NB), :],
            send_sem=hs.at[e, s, way], recv_sem=hr.at[e, s, way],
            device_id={"sx": sx_dev[way]}, device_id_type=MESH)

    def b_copy(e, s, way, part):
        span = pl.ds(0, 8) if part == 0 else pl.ds(8, 4)
        return pltpu.make_async_remote_copy(
            src_ref=bsend.at[e, s, way, span], dst_ref=brecv.at[e, s, way, span],
            send_sem=hs.at[e, s, 2 + 2 * part + way], recv_sem=hr.at[e, s, 2 + 2 * part + way],
            device_id={"sy": sy_dev[way]}, device_id_type=MESH)

    def pair(part, p):
        return (W + p, W + 8 + p) if part == 0 else (p, W + NA + p)

    def swap(tile):
        return pltpu.roll(tile, 4, 0)

    def b_send(ref, at, e, s, part):
        base = 0 if part == 0 else 8

        def pack(p):
            one, two = pair(part, p)
            bsend[e, s, 0, base + p] = jnp.where(
                low, ref[at, s, one, 0:8, :], swap(ref[at, s, two, 0:8, :]))
            bsend[e, s, 1, base + p] = jnp.where(
                low, swap(ref[at, s, one, NB - 8:NB, :]), ref[at, s, two, NB - 8:NB, :])
        loop(8 if part == 0 else 4, pack)
        for way in range(2):
            b_copy(e, s, way, part).start()

    def b_recv(ref, at, e, s, part):
        base = 0 if part == 0 else 8
        for way in range(2):
            b_copy(e, s, way, part).wait_recv()

        def unpack(p):
            one, two = pair(part, p)
            above = brecv[e, s, 0, base + p]
            below = brecv[e, s, 1, base + p]
            ref[at, s, one, NB:PB, :] = jnp.where(low, above, swap(below))
            ref[at, s, two, NB:PB, :] = jnp.where(low, swap(above), below)
        loop(8 if part == 0 else 4, unpack)

    def halo_send(ref, at, e, s, width):
        for way in range(2):
            a_copy(ref, at, e, s, way, width).start()
        b_send(ref, at, e, s, 0)

    def a_wait(ref, at, e, s, width):
        for way in range(2):
            a_copy(ref, at, e, s, way, width).wait_recv()
        b_send(ref, at, e, s, 1)

    def f_copy(sw, s, d):
        return pltpu.make_async_remote_copy(
            src_ref=fsend.at[sw, s, peers[d]], dst_ref=frecv.at[sw, s, d - 1],
            send_sem=as_.at[sw, s, 0, d - 1], recv_sem=ar.at[sw, s, 0, d - 1],
            device_id={"node": peers[d]}, device_id_type=MESH)

    def r_copy(sw, s, d):
        return pltpu.make_async_remote_copy(
            src_ref=rsend.at[sw, s, d], dst_ref=rrecv.at[sw, s, d - 1],
            send_sem=as_.at[sw, s, 1, d - 1], recv_sem=ar.at[sw, s, 1, d - 1],
            device_id={"node": peers[d]}, device_id_type=MESH)

    def start_copy(q):
        return pltpu.make_async_remote_copy(
            src_ref=prev.at[0, :, pl.ds(SLAB * q, SLAB)], dst_ref=start,
            send_sem=ss.at[q], recv_sem=sr.at[0],
            device_id={"node": q}, device_id_type=MESH)

    def around(field):
        total = pltpu.roll(field, 1, 0) + pltpu.roll(field, PB - 1, 0)
        return total + (pltpu.roll(field, 1, 1) + pltpu.roll(field, NC - 1, 1))

    def turn(src, src_at, dst, dst_at, sw, s, first, last):
        def plane(i):
            a = first + i
            total = around(src[src_at, s, a]) + (src[src_at, s, a - 1] + src[src_at, s, a + 1])
            dst[dst_at, s, a] = g[sw, s, a] + ratio[s] * total
        loop(last - first, plane)

    def fill(a):
        for s in range(2):
            x[0, s, W + a, 0:NB, :] = prev[0, s, a]
    loop(NA, fill)
    for sw in range(SWEEPS):
        for s in range(2):
            for a in (0, PA - 1):
                g[sw, s, a] = jnp.zeros((PB, NC), jnp.float32)
    pl.semaphore_wait(barrier, len(others))
    for s in range(2):
        halo_send(x, 0, 0, s, W)

    @pl.when(node == NODES - 1)
    def _():
        for q in (1, 0, 2):
            start_copy(q).start()

        def own(a):
            for s in range(2):
                start[s, a] = prev[0, s, NA - SLAB + a]
        loop(SLAB, own)

    def sweep(sw, carry):
        e0 = ROUNDS * sw
        for s in range(2):
            a_wait(x, e0, e0, s, W)
        for s in range(2):
            b_recv(x, e0, e0, s, 0)

        def force(a):
            parts = []
            for s in range(2):
                mid = x[e0, s, W + a]
                total = around(mid)[0:NB] + (
                    x[e0, s, W + a - 1, 0:NB, :] + x[e0, s, W + a + 1, 0:NB, :])
                own = mid[0:NB]
                part = jnp.float32(diffusion_values[s]) * (total - 6.0 * own)
                diff[s, a] = part
                parts.append((own, part))
            (u, du), (v, dv) = parts
            uvv = u * v * v
            rate = feed[a]
            q = a // SLAB
            b = a % SLAB
            fsend[sw, 0, q, b] = du + (rate * (1.0 - u) - uvv)
            fsend[sw, 1, q, b] = dv + (uvv - (rate + kill[a]) * v)
        loop(NA, force)
        for s in range(2):
            for d in (2, 1, 3):
                f_copy(sw, s, d).start()

        @pl.when((sw == 0) & (node != NODES - 1))
        def _():
            start_copy(0).wait_recv()

        for s in range(2):
            for d in (1, 3, 2):
                f_copy(sw, s, d).wait_recv()

            def combine(b):
                forces = [fsend[sw, s, node, b]] + [frecv[sw, s, d - 1, b] for d in (1, 2, 3)]
                base = start[s, b]
                for d in range(NODES):
                    total = base
                    for j in range(NODES):
                        total = total + weights[d][j] * forces[j]
                    rsend[sw, s, d, b] = total
            weights = [[chosen(node, [time_step * qmatrix[(n + d) % NODES][(n - j) % NODES]
                                      for n in range(NODES)]) for j in range(NODES)]
                       for d in range(NODES)]
            loop(SLAB, combine)
            for d in (2, 1, 3):
                r_copy(sw, s, d).start()
        for s in range(2):
            b_recv(x, e0, e0, s, 1)
        for s in range(2):
            for d in (0, 1, 3, 2):
                if d:
                    r_copy(sw, s, d).wait_recv()
                q = sources[d]

                def right(b):
                    value = rsend[sw, s, 0, b] if d == 0 else rrecv[sw, s, d - 1, b]
                    a = q * SLAB + b
                    g[sw, s, W + a, 0:NB, :] = (value - h_tau * diff[s, a]) * inv[s]
                loop(SLAB, right)
            halo_send(g, sw, 2 * ROUNDS + sw, s, W - 1)
        for k in range(ROUNDS):
            e = e0 + k
            for s in range(2):
                if k == 0:
                    eg = 2 * ROUNDS + sw
                    a_wait(g, sw, eg, s, W - 1)
                    b_recv(g, sw, eg, s, 0)
                    b_recv(g, sw, eg, s, 1)
                else:
                    a_wait(x, e, e, s, W)
                    b_recv(x, e, e, s, 0)
                    b_recv(x, e, e, s, 1)
                turn(x, e, t, 0, sw, s, 1, PA - 1)
                turn(t, 0, t, 1, sw, s, 2, PA - 2)
                turn(t, 1, t, 0, sw, s, 3, PA - 3)
                turn(t, 0, x, e + 1, sw, s, 4, PA - 4)
                if k < ROUNDS - 1:
                    halo_send(x, e + 1, e + 1, s, W)
                else:
                    @pl.when(sw < SWEEPS - 1)
                    def _():
                        halo_send(x, e + 1, e + 1, s, W)
        return carry
    lax.fori_loop(0, SWEEPS, sweep, 0)

    def drain(a):
        for s in range(2):
            out[0, s, a] = x[SWEEPS * ROUNDS, s, W + a, 0:NB, :]
    loop(NA, drain)

    for e in range(2 * ROUNDS + SWEEPS):
        for s in range(2):
            for way in range(2):
                if e < 2 * ROUNDS:
                    a_copy(x, e, e, s, way, W).wait_send()
                else:
                    a_copy(g, e - 2 * ROUNDS, e, s, way, W - 1).wait_send()
                for part in range(2):
                    b_copy(e, s, way, part).wait_send()
    for sw in range(SWEEPS):
        for s in range(2):
            for d in (1, 2, 3):
                f_copy(sw, s, d).wait_send()
                r_copy(sw, s, d).wait_send()

    @pl.when(node == NODES - 1)
    def _():
        for q in range(NODES - 1):
            start_copy(q).wait_send()


def body(previous, feed_rate, kill_rate):
    f32 = jnp.float32
    exchanges = SWEEPS * (ROUNDS + 1)
    dma = pltpu.SemaphoreType.DMA
    return pl.pallas_call(
        kernel,
        out_shape=jax.ShapeDtypeStruct(previous.shape, f32),
        in_specs=[pl.BlockSpec(memory_space=pltpu.VMEM)] * 3,
        out_specs=pl.BlockSpec(memory_space=pltpu.VMEM),
        scratch_shapes=[
            pltpu.VMEM((SWEEPS * ROUNDS + 1, 2, PA, PB, NC), f32),
            pltpu.VMEM((SWEEPS, 2, PA, PB, NC), f32),
            pltpu.VMEM((2, 2, PA, PB, NC), f32),
            pltpu.VMEM((2, NA, NB, NC), f32),
            pltpu.VMEM((SWEEPS, 2, NODES, SLAB, NB, NC), f32),
            pltpu.VMEM((SWEEPS, 2, NODES - 1, SLAB, NB, NC), f32),
            pltpu.VMEM((SWEEPS, 2, NODES, SLAB, NB, NC), f32),
            pltpu.VMEM((SWEEPS, 2, NODES - 1, SLAB, NB, NC), f32),
            pltpu.VMEM((2, SLAB, NB, NC), f32),
            pltpu.VMEM((exchanges, 2, 2, 12, 8, NC), f32),
            pltpu.VMEM((exchanges, 2, 2, 12, 8, NC), f32),
            dma((exchanges, 2, 6)), dma((exchanges, 2, 6)),
            dma((SWEEPS, 2, 2, 3)), dma((SWEEPS, 2, 2, 3)),
            dma((3,)), dma((1,)),
        ],
        compiler_params=pltpu.CompilerParams(
            collective_id=0, has_side_effects=True, vmem_limit_bytes=56 * 1024 * 1024),
    )(previous, feed_rate, kill_rate)


def solution(mesh):
    return jax.shard_map(
        body,
        mesh=mesh,
        in_specs=(P("node", None, "sx", "sy", None), P("sx", "sy", None), P("sx", "sy", None)),
        out_specs=P("node", None, "sx", "sy", None),
        check_vma=False,
    )
```

time: 482 us -> 251 us (0.52)
  Pallas kernels: 0 us -> 248 us
  waiting for transfers between devices: 191 us -> 0 us
  starting transfers between devices: 136 us -> 0 us
  blocking collectives: 52 us -> 0 us
  other arithmetic: 46.1 us -> 0 us
  local copies, waits for them, and re-layouts: 37.5 us -> 2.31 us
  between operations: 14.2 us -> 0.01 us
    pallas_call x0 -> x1, Pallas kernels: none -> 248 us  [body(): pl.pallas_call(kernel, out_shape=jax.ShapeDtypeStruct(previous.shape, f32...]
    ppermute x64 -> x0, starting transfers between devices: 131 us -> none  [the longest x24 74.2 us: padded_3(): lax.ppermute(lax.slice_in_dim(block, 0, width, axis=dim), axis, backward)]
    ppermute x64 -> x0, waiting for transfers between devices: 119 us -> none  [the longest x24 63.7 us: padded_3(): lax.ppermute(lax.slice_in_dim(block, block.shape[dim] - width, None, axis...]
    all_to_all x1 -> x0, waiting for transfers between devices: 72.7 us -> none  [sent_and_summed(): blocks = lax.all_to_all(split_up(array, dim, count), axis, 0, 0, tiled=True)]
    all_to_all x1 -> x0, blocking collectives: 52 us -> none  [sent_and_summed(): blocks = lax.all_to_all(split_up(array, dim, count), axis, 0, 0, tiled=True)]
    slice x84 -> x0, local copies, waits for them, and re-layouts: 21.9 us -> none  [the longest x52 18.7 us: beside(): return total + jnp.roll(center, 1, 3) + jnp.roll(center, -1, 3)]
    div x24 -> x0, other arithmetic: 21.9 us -> none  [the longest x12 12.1 us: double_turn(): midway = (extended + coef * beside(beside_all)) / (1.0 + 6.0 * coef)]
    while x48 -> x0, local copies, waits for them, and re-layouts: 10.8 us -> none
  transfers between devices with their start and end apart: 66 -> 0, of which waited for: 54 -> 0; matrix products, arithmetic and copies ran while one was open for 3% -> 0% of each run, Pallas kernels for 0% -> 0%
where the time goes in v1:
time: 251 us; the launch traced here: 250 us
  Pallas kernels  248 us (99%)
    pallas_call x1, Pallas kernels, body(): pl.pallas_call(kernel, out_shape=jax.ShapeDtypeStruct(previous.shape, f32...  248 us

profile of v1, /device:TPU:1, one launch (start us, length us, event | category | flops | bytes accessed | tf_op | source)
XLA Modules:
  0.0 250.0 jit_solution(4320035102103383361)
XLA Ops:
  0.0 247.7 %shard_map.37 = f32[1,2,16,32,256]{4,3,2,1,0:T(8,128)} custom-call(f32[1,2,16,32,256]{4,3,2,1,0:T(8,128)} %prev.1, f32[16,32,256]{2,1,0:T(8,128)} %feed.1, f32[16,32,256]{2,1,0:T(8,128)} %kill.1), custom_call_target="tpu_custom_call" | custom-call | tf_op jit(solution)/shard_map/pallas_call | solution.py:315
  247.7 2.3 copy.5

commit v2 on v1

--- a/solution.py
+++ b/solution.py
@@ -12,6 +12,7 @@
 PA, PB = NA + 2 * W, NB + 2 * W
 NODES = 4
 SLAB = NA // NODES
+UNROLL = 11
 MESH = pl.DeviceIdType.MESH
 
 radau_points = [0.088587959512704, 0.409466864440735, 0.787659461760847, 1.0]
@@ -51,7 +52,7 @@
     return result
 
 
-def kernel(prev, feed, kill, out, x, g, t, diff, fsend, frecv, rsend, rrecv, start,
+def kernel(prev, feed, kill, out, x, g, t0, t1, diff, fsend, frecv, rsend, rrecv, start,
            bsend, brecv, hs, hr, as_, ar, ss, sr):
     node = lax.axis_index("node")
     sx = lax.axis_index("sx")
@@ -77,11 +78,18 @@
 
     low = lax.broadcasted_iota(jnp.int32, (8, NC), 0) < W
 
-    def loop(count, fn):
+    def loop(count, fn, unroll=1):
         def step(i, carry):
-            fn(i)
+            for k in range(unroll):
+                fn(i * unroll + k)
             return carry
-        lax.fori_loop(0, count, step, 0)
+        trips = count // unroll
+        if trips == 1:
+            step(0, 0)
+        else:
+            lax.fori_loop(0, trips, step, 0)
+        for k in range(trips * unroll, count):
+            fn(k)
 
     def a_copy(ref, at, e, s, way, width):
         src = W if way == 0 else W + NA - width
@@ -114,7 +122,7 @@
                 low, ref[at, s, one, 0:8, :], swap(ref[at, s, two, 0:8, :]))
             bsend[e, s, 1, base + p] = jnp.where(
                 low, swap(ref[at, s, one, NB - 8:NB, :]), ref[at, s, two, NB - 8:NB, :])
-        loop(8 if part == 0 else 4, pack)
+        loop(8 if part == 0 else 4, pack, 4)
         for way in range(2):
             b_copy(e, s, way, part).start()
 
@@ -129,7 +137,7 @@
             below = brecv[e, s, 1, base + p]
             ref[at, s, one, NB:PB, :] = jnp.where(low, above, swap(below))
             ref[at, s, two, NB:PB, :] = jnp.where(low, swap(above), below)
-        loop(8 if part == 0 else 4, unpack)
+        loop(8 if part == 0 else 4, unpack, 4)
 
     def halo_send(ref, at, e, s, width):
         for way in range(2):
@@ -163,17 +171,28 @@
         total = pltpu.roll(field, 1, 0) + pltpu.roll(field, PB - 1, 0)
         return total + (pltpu.roll(field, 1, 1) + pltpu.roll(field, NC - 1, 1))
 
-    def turn(src, src_at, dst, dst_at, sw, s, first, last):
-        def plane(i):
-            a = first + i
-            total = around(src[src_at, s, a]) + (src[src_at, s, a - 1] + src[src_at, s, a + 1])
-            dst[dst_at, s, a] = g[sw, s, a] + ratio[s] * total
-        loop(last - first, plane)
+    def turn(src, dst, sw, s, first, last):
+        def planes(i, count):
+            at = [first + i + k for k in range(-1, count + 1)]
+            rows = [src[a] for a in at]
+            sides = [around(row) for row in rows[1:-1]]
+            for k in range(count):
+                total = sides[k] + (rows[k] + rows[k + 2])
+                dst[at[k + 1]] = g[sw, s, at[k + 1]] + ratio[s] * total
+
+        def step(i, carry):
+            planes(i * UNROLL, UNROLL)
+            return carry
+        count = last - first
+        trips = count // UNROLL
+        lax.fori_loop(0, trips, step, 0)
+        if count % UNROLL:
+            planes(trips * UNROLL, count % UNROLL)
 
     def fill(a):
         for s in range(2):
             x[0, s, W + a, 0:NB, :] = prev[0, s, a]
-    loop(NA, fill)
+    loop(NA, fill, 4)
     for sw in range(SWEEPS):
         for s in range(2):
             for a in (0, PA - 1):
@@ -216,7 +235,7 @@
             b = a % SLAB
             fsend[sw, 0, q, b] = du + (rate * (1.0 - u) - uvv)
             fsend[sw, 1, q, b] = dv + (uvv - (rate + kill[a]) * v)
-        loop(NA, force)
+        loop(NA, force, 4)
         for s in range(2):
             for d in (2, 1, 3):
                 f_copy(sw, s, d).start()
@@ -240,7 +259,7 @@
             weights = [[chosen(node, [time_step * qmatrix[(n + d) % NODES][(n - j) % NODES]
                                       for n in range(NODES)]) for j in range(NODES)]
                        for d in range(NODES)]
-            loop(SLAB, combine)
+            loop(SLAB, combine, 2)
             for d in (2, 1, 3):
                 r_copy(sw, s, d).start()
         for s in range(2):
@@ -255,7 +274,7 @@
                     value = rsend[sw, s, 0, b] if d == 0 else rrecv[sw, s, d - 1, b]
                     a = q * SLAB + b
                     g[sw, s, W + a, 0:NB, :] = (value - h_tau * diff[s, a]) * inv[s]
-                loop(SLAB, right)
+                loop(SLAB, right, 4)
             halo_send(g, sw, 2 * ROUNDS + sw, s, W - 1)
         for k in range(ROUNDS):
             e = e0 + k
@@ -269,10 +288,10 @@
                     a_wait(x, e, e, s, W)
                     b_recv(x, e, e, s, 0)
                     b_recv(x, e, e, s, 1)
-                turn(x, e, t, 0, sw, s, 1, PA - 1)
-                turn(t, 0, t, 1, sw, s, 2, PA - 2)
-                turn(t, 1, t, 0, sw, s, 3, PA - 3)
-                turn(t, 0, x, e + 1, sw, s, 4, PA - 4)
+                turn(x.at[e, s], t0, sw, s, 1, PA - 1)
+                turn(t0, t1, sw, s, 2, PA - 2)
+                turn(t1, t0, sw, s, 3, PA - 3)
+                turn(t0, x.at[e + 1, s], sw, s, 4, PA - 4)
                 if k < ROUNDS - 1:
                     halo_send(x, e + 1, e + 1, s, W)
                 else:
@@ -285,7 +304,7 @@
     def drain(a):
         for s in range(2):
             out[0, s, a] = x[SWEEPS * ROUNDS, s, W + a, 0:NB, :]
-    loop(NA, drain)
+    loop(NA, drain, 4)
 
     for e in range(2 * ROUNDS + SWEEPS):
         for s in range(2):
@@ -320,7 +339,8 @@
         scratch_shapes=[
             pltpu.VMEM((SWEEPS * ROUNDS + 1, 2, PA, PB, NC), f32),
             pltpu.VMEM((SWEEPS, 2, PA, PB, NC), f32),
-            pltpu.VMEM((2, 2, PA, PB, NC), f32),
+            pltpu.VMEM((PA, PB, NC), f32),
+            pltpu.VMEM((PA, PB, NC), f32),
             pltpu.VMEM((2, NA, NB, NC), f32),
             pltpu.VMEM((SWEEPS, 2, NODES, SLAB, NB, NC), f32),
             pltpu.VMEM((SWEEPS, 2, NODES - 1, SLAB, NB, NC), f32),

time: 251 us -> 192 us (0.76)
  Pallas kernels: 248 us -> 190 us
    pallas_call x1, Pallas kernels: 248 us -> 190 us  [body(): pl.pallas_call(kernel, out_shape=jax.ShapeDtypeStruct(previous.shape, f32...]
where the time goes in v2:
time: 192 us
  Pallas kernels  190 us (99%)
  local copies, waits for them, and re-layouts  2.31 us (1%)
    pallas_call x1, Pallas kernels, body(): pl.pallas_call(kernel, out_shape=jax.ShapeDtypeStruct(previous.shape, f32...  190 us

profile of v2, /device:TPU:1, one launch (start us, length us, event | category | flops | bytes accessed | tf_op | source)
XLA Modules:
  0.0 192.1 jit_solution(6395749541006349670)
XLA Ops:
  0.0 189.8 %shard_map.37 = f32[1,2,16,32,256]{4,3,2,1,0:T(8,128)} custom-call(f32[1,2,16,32,256]{4,3,2,1,0:T(8,128)} %prev.1, f32[16,32,256]{2,1,0:T(8,128)} %feed.1, f32[16,32,256]{2,1,0:T(8,128)} %kill.1), custom_call_target="tpu_custom_call" | custom-call | tf_op jit(solution)/shard_map/pallas_call | solution.py:334
  189.8 2.3 %copy.5 = f32[1,2,16,32,256]{4,3,2,1,0:T(8,128)} copy(f32[1,2,16,32,256]{4,3,2,1,0:T(8,128)} %shard_map.37) | data formatting | bytes 2097152

commit v3 on v2

v3 whole, which is shorter than its diff:
```python
import jax
import jax.numpy as jnp
from jax import lax
from jax.experimental import pallas as pl
from jax.experimental.pallas import tpu as pltpu
from jax.sharding import PartitionSpec as P

SWEEPS = 2
W = 4
NA, NB, NC = 16, 32, 256
PA, PB = NA + 2 * W, NB + 2 * W
NODES = 4
SLAB = NA // NODES
XS = 3
LAST = XS * SWEEPS
MESH = pl.DeviceIdType.MESH

radau_points = [0.088587959512704, 0.409466864440735, 0.787659461760847, 1.0]
time_step = 4.0
diffusion_values = [1.0, 0.5]


def collocation():
    count = len(radau_points)
    table = []
    for row in range(count):
        table.append([0.0] * count)
    for column in range(count):
        poly = [1.0]
        denom = 1.0
        for other in range(count):
            if other != column:
                longer = [0.0] * (len(poly) + 1)
                for place in range(len(poly)):
                    longer[place + 1] = longer[place + 1] + poly[place]
                    longer[place] = longer[place] - radau_points[other] * poly[place]
                poly = longer
                denom = denom * (radau_points[column] - radau_points[other])
        for row in range(count):
            point = radau_points[row]
            total = 0.0
            for place in range(len(poly)):
                total = total + poly[place] * point ** (place + 1) / (place + 1)
            table[row][column] = total / denom
    return table


def chosen(index, values):
    result = jnp.float32(values[-1])
    for place in range(len(values) - 2, -1, -1):
        result = jnp.where(index == place, jnp.float32(values[place]), result)
    return result


def kernel(prev, feed, kill, out, x, g, t0, t1, drop, fsend, frecv, rsend, rrecv, start,
           bsend, brecv, csend, crecv, rbuf, hs, hr, as_, ar, ss, sr):
    node = lax.axis_index("node")
    sx = lax.axis_index("sx")
    sy = lax.axis_index("sy")
    nsx = lax.axis_size("sx")
    nsy = lax.axis_size("sy")
    y = lax.rem(sx, 4)
    edge = [y == 0, y == 3]
    inside = [y != 0, y != 3]
    sx_dev = [lax.rem(sx + nsx - 1, nsx), lax.rem(sx + 1, nsx)]
    in_dev = [lax.rem(sx + 3, nsx), lax.rem(sx + nsx - 3, nsx)]
    out_dev = [lax.rem(sx + nsx - 4, nsx), lax.rem(sx + 4, nsx)]
    sy_dev = [lax.rem(sy + nsy - 1, nsy), lax.rem(sy + 1, nsy)]
    peers = {d: lax.rem(node + d, NODES) for d in range(NODES)}
    sources = {d: lax.rem(node + NODES - d, NODES) for d in range(NODES)}

    qmatrix = collocation()
    coefs = [[time_step * p * d for p in radau_points] for d in diffusion_values]
    inv = [chosen(node, [1.0 / (1.0 + 6.0 * c) for c in cs]) for cs in coefs]
    ratio = [chosen(node, [c / (1.0 + 6.0 * c) for c in cs]) for cs in coefs]
    weights = [[chosen(node, [time_step * qmatrix[(n + d) % NODES][(n - j) % NODES]
                              for n in range(NODES)]) for j in range(NODES)]
               for d in range(NODES)]

    low = lax.broadcasted_iota(jnp.int32, (8, NC), 0) < 4
    barrier = pltpu.get_barrier_semaphore()
    others = [{"node": peers[d]} for d in (1, 2, 3)]
    others += [{"sx": p} for p in sx_dev + in_dev + out_dev] + [{"sy": p} for p in sy_dev]
    others += [{"sx": p, "sy": q} for p in sx_dev for q in sy_dev]
    for other in others:
        pl.semaphore_signal(barrier, inc=1, device_id=other, device_id_type=MESH)

    def loop(count, fn, unroll=1):
        def step(i, carry):
            for k in range(unroll):
                fn(i * unroll + k)
            return carry
        lax.fori_loop(0, count // unroll, step, 0)

    def remote(src, dst, e, s, slot, device):
        return pltpu.make_async_remote_copy(
            src_ref=src, dst_ref=dst, send_sem=hs.at[e, s, slot], recv_sem=hr.at[e, s, slot],
            device_id=device, device_id_type=MESH)

    def span(way, first, last):
        if way == 0:
            return W + first - 1, W + NA + first - 1, last - first + 1
        return W + NA - last, W - last, last - first + 1

    def relayed(ex):
        return (ex[4] - ex[3] + 1) // 2

    def a_copy(ex, s, way, first, last, slot):
        ref, at, e = ex[:3]
        src, dst, count = span(way, first, last)
        return remote(ref.at[at, s, pl.ds(src, count), pl.ds(0, NB), :],
                      ref.at[at, s, pl.ds(dst, count), pl.ds(0, NB), :],
                      e, s, slot + way, {"sx": sx_dev[way]})

    def relay_in(ex, s, way):
        ref, at, e, first, last = ex
        src, dst, count = span(way, last - relayed(ex) + 1, last)
        return remote(ref.at[at, s, pl.ds(src, count), pl.ds(0, NB), :],
                      rbuf.at[e, s, pl.ds(0, count)], e, s, 2, {"sx": in_dev[way]})

    def relay_out(ex, s, way):
        ref, at, e, first, last = ex
        src, dst, count = span(way, last - relayed(ex) + 1, last)
        return remote(rbuf.at[e, s, pl.ds(0, count)],
                      ref.at[at, s, pl.ds(dst, count), pl.ds(0, NB), :],
                      e, s, 3, {"sx": out_dev[way]})

    def whole(ex, s, way):
        return a_copy(ex, s, way, ex[3], ex[4], 0)

    def direct(ex, s, way):
        return a_copy(ex, s, way, ex[3], ex[4] - relayed(ex), 0)

    def layer(ex, s, way):
        return a_copy(ex, s, way, 1, 1, 10)

    def b_copy(ex, s, way):
        e = ex[2]
        return remote(bsend.at[e, s, way], brecv.at[e, s, way],
                      e, s, 4 + way, {"sy": sy_dev[way]})

    def c_copy(ex, s, n):
        e = ex[2]
        return remote(csend.at[e, s, n], crecv.at[e, s, n],
                      e, s, 6 + n, {"sx": sx_dev[n // 2], "sy": sy_dev[n % 2]})

    def swap(tile):
        return pltpu.roll(tile, 4, 0)

    def first_rows(ex, s, one, two):
        ref, at = ex[:2]
        return jnp.where(low, ref[at, s, one, 0:8, :], swap(ref[at, s, two, 0:8, :]))

    def last_rows(ex, s, one, two):
        ref, at = ex[:2]
        return jnp.where(low, swap(ref[at, s, one, NB - 8:NB, :]), ref[at, s, two, NB - 8:NB, :])

    def put_rows(ex, s, one, two, above, below):
        ref, at = ex[:2]
        ref[at, s, one, NB:PB, :] = jnp.where(low, above, swap(below))
        ref[at, s, two, NB:PB, :] = jnp.where(low, swap(above), below)

    def b_send(ex, s):
        e = ex[2]

        def pack(p):
            bsend[e, s, 0, p] = first_rows(ex, s, W + p, W + 8 + p)
            bsend[e, s, 1, p] = last_rows(ex, s, W + p, W + 8 + p)
        loop(8, pack, 4)
        for way in range(2):
            b_copy(ex, s, way).start()

    def b_recv(ex, s):
        e = ex[2]
        for way in range(2):
            b_copy(ex, s, way).wait_recv()

        def unpack(p):
            put_rows(ex, s, W + p, W + 8 + p, brecv[e, s, 0, p], brecv[e, s, 1, p])
        loop(8, unpack, 4)

    def c_send(ex, s):
        e = ex[2]
        for n in range(4):
            base = W if n < 2 else NA
            for p in range(2):
                rows = first_rows if n % 2 == 0 else last_rows
                csend[e, s, n, p] = rows(ex, s, base + p, base + p + 2)
            c_copy(ex, s, n).start()

    def c_recv(ex, s):
        e = ex[2]
        for n in range(4):
            c_copy(ex, s, n).wait_recv()
        for way in range(2):
            base = W + NA if way == 0 else 0
            for p in range(2):
                put_rows(ex, s, base + p, base + p + 2,
                         crecv[e, s, 2 * way, p], crecv[e, s, 2 * way + 1, p])

    def relay(ex, s):
        for way in range(2):
            @pl.when(edge[1 - way])
            def _():
                relay_in(ex, s, way).wait_recv()
                relay_out(ex, s, way).start()

    def halo_send(ex, s):
        if ex[3] > 1:
            for way in range(2):
                layer(ex, s, way).start()
            b_send(ex, s)
        for way in range(2):
            @pl.when(edge[way])
            def _():
                relay_in(ex, s, way).start()
                direct(ex, s, way).start()

            @pl.when(inside[way])
            def _():
                whole(ex, s, way).start()
        c_send(ex, s)
        if ex[3] == 1:
            b_send(ex, s)

    def near_wait(ex, s):
        for way in range(2):
            layer(ex, s, way).wait_recv()
        b_recv(ex, s)

    def a_wait(ex, s):
        for way in range(2):
            @pl.when(edge[1 - way])
            def _():
                direct(ex, s, way).wait_recv()
                relay_out(ex, s, way).wait_recv()

            @pl.when(inside[1 - way])
            def _():
                whole(ex, s, way).wait_recv()

    def b_wait(ex, s):
        if ex[3] == 1:
            b_recv(ex, s)
        c_recv(ex, s)

    def sent(ex, s):
        for way in range(2):
            if ex[3] > 1:
                layer(ex, s, way).wait_send()

            @pl.when(edge[way])
            def _():
                relay_in(ex, s, way).wait_send()
                direct(ex, s, way).wait_send()

            @pl.when(inside[way])
            def _():
                whole(ex, s, way).wait_send()

            @pl.when(edge[1 - way])
            def _():
                relay_out(ex, s, way).wait_send()
        for way in range(2):
            b_copy(ex, s, way).wait_send()
        for n in range(4):
            c_copy(ex, s, n).wait_send()

    def f_copy(sw, s, d):
        return pltpu.make_async_remote_copy(
            src_ref=fsend.at[sw, s, peers[d]], dst_ref=frecv.at[sw, s, d - 1],
            send_sem=as_.at[sw, s, 0, d - 1], recv_sem=ar.at[sw, s, 0, d - 1],
            device_id={"node": peers[d]}, device_id_type=MESH)

    def r_copy(sw, s, d):
        return pltpu.make_async_remote_copy(
            src_ref=rsend.at[sw, s, d], dst_ref=rrecv.at[sw, s, d - 1],
            send_sem=as_.at[sw, s, 1, d - 1], recv_sem=ar.at[sw, s, 1, d - 1],
            device_id={"node": peers[d]}, device_id_type=MESH)

    def start_copy(q):
        return pltpu.make_async_remote_copy(
            src_ref=prev.at[0, :, pl.ds(SLAB * q, SLAB)], dst_ref=start,
            send_sem=ss.at[q], recv_sem=sr.at[0],
            device_id={"node": q}, device_id_type=MESH)

    def around(field):
        total = pltpu.roll(field, 1, 0) + pltpu.roll(field, PB - 1, 0)
        return total + (pltpu.roll(field, 1, 1) + pltpu.roll(field, NC - 1, 1))

    def turn(src, dst, sw, s, level, rows=PB):
        half = (PA - 2 * level) // 2

        def step(i, carry):
            at = [level + i * half + k for k in range(-1, half + 1)]
            planes = [src[a] for a in at]
            sides = [around(plane)[0:rows] for plane in planes[1:-1]]
            for k in range(half):
                total = sides[k] + (planes[k][0:rows] + planes[k + 2][0:rows])
                dst[at[k + 1], 0:rows, :] = g[sw, s, at[k + 1], 0:rows, :] + ratio[s] * total
            return carry
        lax.fori_loop(0, 2, step, 0)

    def fill(a):
        for s in range(2):
            x[0, s, W + a, 0:NB, :] = prev[0, s, a]
    loop(NA, fill, 4)
    for sw in range(SWEEPS):
        for s in range(2):
            for a in (0, PA - 1):
                g[sw, s, a] = jnp.zeros((PB, NC), jnp.float32)
    pl.semaphore_wait(barrier, len(others))
    for s in range(2):
        halo_send((x, 0, 0, 2, W), s)

    @pl.when(node == NODES - 1)
    def _():
        for q in (1, 0, 2):
            start_copy(q).start()

        def own(a):
            for s in range(2):
                start[s, a] = prev[0, s, NA - SLAB + a]
        loop(SLAB, own, 4)

    def sweep(sw, carry):
        e0 = XS * sw
        ex_0 = (x, e0, e0, 2, W)
        exs = [ex_0] + [(x, e0 + k, e0 + k, 1, W) for k in range(1, XS)]
        exs += [(x, e0 + XS, e0 + XS, 2, W)]
        ex_g = (g, sw, LAST + sw, 1, W - 1)
        for s in range(2):
            near_wait(ex_0, s)

        def force(a):
            parts = []
            for s in range(2):
                mid = x[e0, s, W + a]
                total = around(mid)[0:NB] + (
                    x[e0, s, W + a - 1, 0:NB, :] + x[e0, s, W + a + 1, 0:NB, :])
                own = mid[0:NB]
                gap = total - 6.0 * own
                drop[s, a] = ratio[s] * gap
                parts.append((own, jnp.float32(diffusion_values[s]) * gap))
            (u, du), (v, dv) = parts
            uvv = u * v * v
            rate = feed[a]
            return du + (rate * (1.0 - u) - uvv), dv + (uvv - (rate + kill[a]) * v)

        for d in (2, 1, 3, 0):
            def slab(b):
                pair = force(peers[d] * SLAB + b)
                for s in range(2):
                    fsend[sw, s, peers[d], b] = pair[s]
            loop(SLAB, slab, 4)
            if d:
                f_copy(sw, 0, d).start()
        for d in (2, 1, 3):
            f_copy(sw, 1, d).start()

        for s in range(2):
            relay(ex_0, s)

        @pl.when((sw == 0) & (node != NODES - 1))
        def _():
            start_copy(0).wait_recv()

        for s in range(2):
            for d in (1, 3, 2):
                f_copy(sw, s, d).wait_recv()

            def combine(b):
                forces = [fsend[sw, s, node, b]] + [frecv[sw, s, d - 1, b] for d in (1, 2, 3)]
                base = start[s, b]
                for d in range(NODES):
                    total = base
                    for j in range(NODES):
                        total = total + weights[d][j] * forces[j]
                    rsend[sw, s, d, b] = total
            loop(SLAB, combine, 2)
            for d in (2, 1, 3):
                r_copy(sw, s, d).start()

        for s in range(2):
            a_wait(ex_0, s)
        for s in range(2):
            for d in (0, 1, 3, 2):
                if d:
                    r_copy(sw, s, d).wait_recv()
                q = sources[d]

                def right(b):
                    value = rsend[sw, s, 0, b] if d == 0 else rrecv[sw, s, d - 1, b]
                    a = q * SLAB + b
                    g[sw, s, W + a, 0:NB, :] = value * inv[s] - drop[s, a]
                loop(SLAB, right, 4)
            halo_send(ex_g, s)
        for s in range(2):
            relay(ex_g, s)

        for k in range(XS):
            now = ex_g if k == 0 else exs[k]
            for s in range(2):
                a_wait(now, s)
                if s == 0 and k > 0:
                    relay(now, 1)
                if s == 1 and k < XS - 1:
                    relay(exs[k + 1], 0)
                b_wait(now, s)
                if k == 0:
                    b_wait(ex_0, s)
                turn(x.at[e0 + k, s], t0, sw, s, 1)
                turn(t0, t1, sw, s, 2)
                turn(t1, t0, sw, s, 3)
                turn(t0, x.at[e0 + k + 1, s], sw, s, 4, NB)
                if k < XS - 1:
                    halo_send(exs[k + 1], s)
                else:
                    @pl.when(sw < SWEEPS - 1)
                    def _():
                        halo_send(exs[XS], s)
        return carry
    lax.fori_loop(0, SWEEPS, sweep, 0)

    def drain(a):
        for s in range(2):
            out[0, s, a] = x[LAST, s, W + a, 0:NB, :]
    loop(NA, drain, 4)

    for s in range(2):
        for sw in range(SWEEPS):
            sent((g, sw, LAST + sw, 1, W - 1), s)
            sent((x, XS * sw, XS * sw, 2, W), s)
            for k in range(1, XS):
                sent((x, XS * sw + k, XS * sw + k, 1, W), s)
            for d in (1, 2, 3):
                f_copy(sw, s, d).wait_send()
                r_copy(sw, s, d).wait_send()

    @pl.when(node == NODES - 1)
    def _():
        for q in range(NODES - 1):
            start_copy(q).wait_send()


def body(previous, feed_rate, kill_rate):
    f32 = jnp.float32
    exchanges = LAST + SWEEPS
    dma = pltpu.SemaphoreType.DMA
    return pl.pallas_call(
        kernel,
        out_shape=jax.ShapeDtypeStruct(previous.shape, f32),
        in_specs=[pl.BlockSpec(memory_space=pltpu.VMEM)] * 3,
        out_specs=pl.BlockSpec(memory_space=pltpu.VMEM),
        scratch_shapes=[
            pltpu.VMEM((LAST + 1, 2, PA, PB, NC), f32),
            pltpu.VMEM((SWEEPS, 2, PA, PB, NC), f32),
            pltpu.VMEM((PA, PB, NC), f32),
            pltpu.VMEM((PA, PB, NC), f32),
            pltpu.VMEM((2, NA, NB, NC), f32),
            pltpu.VMEM((SWEEPS, 2, NODES, SLAB, NB, NC), f32),
            pltpu.VMEM((SWEEPS, 2, NODES - 1, SLAB, NB, NC), f32),
            pltpu.VMEM((SWEEPS, 2, NODES, SLAB, NB, NC), f32),
            pltpu.VMEM((SWEEPS, 2, NODES - 1, SLAB, NB, NC), f32),
            pltpu.VMEM((2, SLAB, NB, NC), f32),
            pltpu.VMEM((exchanges, 2, 2, 8, 8, NC), f32),
            pltpu.VMEM((exchanges, 2, 2, 8, 8, NC), f32),
            pltpu.VMEM((exchanges, 2, 4, 2, 8, NC), f32),
            pltpu.VMEM((exchanges, 2, 4, 2, 8, NC), f32),
            pltpu.VMEM((exchanges, 2, W // 2, NB, NC), f32),
            dma((exchanges, 2, 12)), dma((exchanges, 2, 12)),
            dma((SWEEPS, 2, 2, 3)), dma((SWEEPS, 2, 2, 3)),
            dma((3,)), dma((1,)),
        ],
        compiler_params=pltpu.CompilerParams(
            collective_id=0, has_side_effects=True, vmem_limit_bytes=56 * 1024 * 1024),
    )(previous, feed_rate, kill_rate)


def solution(mesh):
    return jax.shard_map(
        body,
        mesh=mesh,
        in_specs=(P("node", None, "sx", "sy", None), P("sx", "sy", None), P("sx", "sy", None)),
        out_specs=P("node", None, "sx", "sy", None),
        check_vma=False,
    )
```

time: 192 us -> 169 us (0.88); the launches traced: 192 us -> 166 us
  Pallas kernels: 190 us -> 164 us
    pallas_call x1, Pallas kernels: 190 us -> 164 us  [body(): pl.pallas_call(kernel, out_shape=jax.ShapeDtypeStruct(previous.shape, f32...]
where the time goes in v3:
time: 169 us; the launch traced here: 166 us
  Pallas kernels  164 us (97%)
  local copies, waits for them, and re-layouts  2.31 us (1%)
    pallas_call x1, Pallas kernels, body(): pl.pallas_call(kernel, out_shape=jax.ShapeDtypeStruct(previous.shape, f32...  164 us

profile of v3, /device:TPU:1, one launch (start us, length us, event | category | flops | bytes accessed | tf_op | source)
XLA Modules:
  0.0 166.2 jit_solution(6727450783669183868)
XLA Ops:
  0.0 163.9 %shard_map.37 = f32[1,2,16,32,256]{4,3,2,1,0:T(8,128)} custom-call(f32[1,2,16,32,256]{4,3,2,1,0:T(8,128)} %prev.1, f32[16,32,256]{2,1,0:T(8,128)} %feed.1, f32[16,32,256]{2,1,0:T(8,128)} %kill.1), custom_call_target="tpu_custom_call" | custom-call | tf_op jit(solution)/shard_map/pallas_call | solution.py:450
  163.9 2.3 %copy.5 = f32[1,2,16,32,256]{4,3,2,1,0:T(8,128)} copy(f32[1,2,16,32,256]{4,3,2,1,0:T(8,128)} %shard_map.37) | data formatting | bytes 2097152

commit v4 on v3

--- a/solution.py
+++ b/solution.py
@@ -103,7 +103,7 @@
         return W + NA - last, W - last, last - first + 1
 
     def relayed(ex):
-        return (ex[4] - ex[3] + 1) // 2
+        return 2
 
     def a_copy(ex, s, way, first, last, slot):
         ref, at, e = ex[:3]
@@ -239,11 +239,6 @@
             def _():
                 whole(ex, s, way).wait_recv()
 
-    def b_wait(ex, s):
-        if ex[3] == 1:
-            b_recv(ex, s)
-        c_recv(ex, s)
-
     def sent(ex, s):
         for way in range(2):
             if ex[3] > 1:
@@ -288,18 +283,28 @@
         total = pltpu.roll(field, 1, 0) + pltpu.roll(field, PB - 1, 0)
         return total + (pltpu.roll(field, 1, 1) + pltpu.roll(field, NC - 1, 1))
 
-    def turn(src, dst, sw, s, level, rows=PB):
-        half = (PA - 2 * level) // 2
+    def advance(src, dst, sw, s, base, groups, rows):
+        held = {}
+        for first, count in groups:
+            for a in range(first - 1, first + count + 1):
+                if a not in held:
+                    held[a] = src[base + a]
+        sides = {a: around(held[a])[0:rows] for first, count in groups
+                 for a in range(first, first + count)}
+        for a, side in sides.items():
+            total = side + (held[a - 1][0:rows] + held[a + 1][0:rows])
+            dst[base + a, 0:rows, :] = g[sw, s, base + a, 0:rows, :] + ratio[s] * total
+
+    def inner(src, dst, sw, s, level, rows=PB):
+        half = NA // 2 - level
 
         def step(i, carry):
-            at = [level + i * half + k for k in range(-1, half + 1)]
-            planes = [src[a] for a in at]
-            sides = [around(plane)[0:rows] for plane in planes[1:-1]]
-            for k in range(half):
-                total = sides[k] + (planes[k][0:rows] + planes[k + 2][0:rows])
-                dst[at[k + 1], 0:rows, :] = g[sw, s, at[k + 1], 0:rows, :] + ratio[s] * total
+            advance(src, dst, sw, s, W + level + i * half, [(0, half)], rows)
             return carry
         lax.fori_loop(0, 2, step, 0)
+
+    def outer(src, dst, sw, s, level, rows=PB):
+        advance(src, dst, sw, s, 0, [(level, W), (PA - W - level, W)], rows)
 
     def fill(a):
         for s in range(2):
@@ -401,18 +406,22 @@
         for k in range(XS):
             now = ex_g if k == 0 else exs[k]
             for s in range(2):
-                a_wait(now, s)
-                if s == 0 and k > 0:
-                    relay(now, 1)
-                if s == 1 and k < XS - 1:
-                    relay(exs[k + 1], 0)
-                b_wait(now, s)
-                if k == 0:
-                    b_wait(ex_0, s)
-                turn(x.at[e0 + k, s], t0, sw, s, 1)
-                turn(t0, t1, sw, s, 2)
-                turn(t1, t0, sw, s, 3)
-                turn(t0, x.at[e0 + k + 1, s], sw, s, 4, NB)
+                b_recv(now, s)
+                src, dst = x.at[e0 + k, s], x.at[e0 + k + 1, s]
+                for part in (inner, outer):
+                    if part is outer:
+                        if s == 0 and k > 0:
+                            relay(now, 1)
+                        if s == 1 and k < XS - 1:
+                            relay(exs[k + 1], 0)
+                        a_wait(now, s)
+                        c_recv(now, s)
+                        if k == 0:
+                            c_recv(ex_0, s)
+                    part(src, t0, sw, s, 1)
+                    part(t0, t1, sw, s, 2)
+                    part(t1, t0, sw, s, 3)
+                    part(t0, dst, sw, s, 4, NB)
                 if k < XS - 1:
                     halo_send(exs[k + 1], s)
                 else:

time: 169 us -> 159 us (0.941); the launches traced: 166 us -> 159 us
  Pallas kernels: 164 us -> 157 us
    pallas_call x1, Pallas kernels: 164 us -> 157 us  [body(): pl.pallas_call(kernel, out_shape=jax.ShapeDtypeStruct(previous.shape, f32...]
where the time goes in v4:
time: 159 us
  Pallas kernels  157 us (99%)
  local copies, waits for them, and re-layouts  2.31 us (1%)
    pallas_call x1, Pallas kernels, body(): pl.pallas_call(kernel, out_shape=jax.ShapeDtypeStruct(previous.shape, f32...  157 us

profile of v4, /device:TPU:1, one launch (start us, length us, event | category | flops | bytes accessed | tf_op | source)
XLA Modules:
  0.0 159.3 jit_solution(5936334894711722516)
XLA Ops:
  0.0 157.0 %shard_map.37 = f32[1,2,16,32,256]{4,3,2,1,0:T(8,128)} custom-call(f32[1,2,16,32,256]{4,3,2,1,0:T(8,128)} %prev.1, f32[16,32,256]{2,1,0:T(8,128)} %feed.1, f32[16,32,256]{2,1,0:T(8,128)} %kill.1), custom_call_target="tpu_custom_call" | custom-call | tf_op jit(solution)/shard_map/pallas_call | solution.py:459
  157.0 2.3 %copy.5 = f32[1,2,16,32,256]{4,3,2,1,0:T(8,128)} copy(f32[1,2,16,32,256]{4,3,2,1,0:T(8,128)} %shard_map.37) | data formatting | bytes 2097152

commit v5 on v4

--- a/solution.py
+++ b/solution.py
@@ -400,8 +400,8 @@
                     g[sw, s, W + a, 0:NB, :] = value * inv[s] - drop[s, a]
                 loop(SLAB, right, 4)
             halo_send(ex_g, s)
-        for s in range(2):
-            relay(ex_g, s)
+            if s == 0:
+                relay(ex_g, 0)
 
         for k in range(XS):
             now = ex_g if k == 0 else exs[k]
@@ -410,7 +410,7 @@
                 src, dst = x.at[e0 + k, s], x.at[e0 + k + 1, s]
                 for part in (inner, outer):
                     if part is outer:
-                        if s == 0 and k > 0:
+                        if s == 0:
                             relay(now, 1)
                         if s == 1 and k < XS - 1:
                             relay(exs[k + 1], 0)

time: 159 us -> 155 us (0.975)
  Pallas kernels: 157 us -> 153 us
    pallas_call x1, Pallas kernels: 157 us -> 153 us  [body(): pl.pallas_call(kernel, out_shape=jax.ShapeDtypeStruct(previous.shape, f32...]
where the time goes in v5:
time: 155 us
  Pallas kernels  153 us (99%)
  local copies, waits for them, and re-layouts  2.31 us (1%)
    pallas_call x1, Pallas kernels, body(): pl.pallas_call(kernel, out_shape=jax.ShapeDtypeStruct(previous.shape, f32...  153 us

profile of v5, /device:TPU:1, one launch (start us, length us, event | category | flops | bytes accessed | tf_op | source)
XLA Modules:
  0.0 155.2 jit_solution(11782365169748261476)
XLA Ops:
  0.0 152.9 %shard_map.37 = f32[1,2,16,32,256]{4,3,2,1,0:T(8,128)} custom-call(f32[1,2,16,32,256]{4,3,2,1,0:T(8,128)} %prev.1, f32[16,32,256]{2,1,0:T(8,128)} %feed.1, f32[16,32,256]{2,1,0:T(8,128)} %kill.1), custom_call_target="tpu_custom_call" | custom-call | tf_op jit(solution)/shard_map/pallas_call | solution.py:459
  152.9 2.3 %copy.5 = f32[1,2,16,32,256]{4,3,2,1,0:T(8,128)} copy(f32[1,2,16,32,256]{4,3,2,1,0:T(8,128)} %shard_map.37) | data formatting | bytes 2097152

commit v6 on v5

--- a/solution.py
+++ b/solution.py
@@ -219,9 +219,9 @@
             @pl.when(inside[way])
             def _():
                 whole(ex, s, way).start()
-        c_send(ex, s)
         if ex[3] == 1:
             b_send(ex, s)
+        c_send(ex, s)
 
     def near_wait(ex, s):
         for way in range(2):
@@ -382,7 +382,7 @@
                     for j in range(NODES):
                         total = total + weights[d][j] * forces[j]
                     rsend[sw, s, d, b] = total
-            loop(SLAB, combine, 2)
+            loop(SLAB, combine, 4)
             for d in (2, 1, 3):
                 r_copy(sw, s, d).start()
 

time: 155 us -> 154 us (level)
  Pallas kernels: 153 us -> 151 us
where the time goes in v6:
time: 154 us
  Pallas kernels  151 us (98%)
  local copies, waits for them, and re-layouts  2.31 us (2%)
    pallas_call x1, Pallas kernels, body(): pl.pallas_call(kernel, out_shape=jax.ShapeDtypeStruct(previous.shape, f32...  151 us

profile of v6, /device:TPU:1, one launch (start us, length us, event | category | flops | bytes accessed | tf_op | source)
XLA Modules:
  0.0 153.7 jit_solution(15364576267606095910)
XLA Ops:
  0.0 151.4 %shard_map.37 = f32[1,2,16,32,256]{4,3,2,1,0:T(8,128)} custom-call(f32[1,2,16,32,256]{4,3,2,1,0:T(8,128)} %prev.1, f32[16,32,256]{2,1,0:T(8,128)} %feed.1, f32[16,32,256]{2,1,0:T(8,128)} %kill.1), custom_call_target="tpu_custom_call" | custom-call | tf_op jit(solution)/shard_map/pallas_call | solution.py:459
  151.4 2.3 %copy.5 = f32[1,2,16,32,256]{4,3,2,1,0:T(8,128)} copy(f32[1,2,16,32,256]{4,3,2,1,0:T(8,128)} %shard_map.37) | data formatting | bytes 2097152
